TPU v7x, 32 devices: a whole 2x2x4 slice. The times are simulated.
32 devices in a mesh: groups: 2 (over x), patch: 16 (over z, y, core).
Axes of the slice: x: 2, y: 2, z: 4, core: 2. Of those that a mesh axis runs over, the one named last changes fastest.
Arguments:
- grid_latents: bfloat16 [32768, 512], P(('groups', 'patch')), parts along dimension 0, may hold values from -6 to 6
- mesh_latents: bfloat16 [16384, 512], P(('groups', 'patch')), parts along dimension 0, may hold values from -6 to 6
- enc_send: int32 [640, 128], P(('groups', 'patch')), parts along dimension 0, may hold values from 0 to 1023
- enc_recv: int32 [640, 128], P(('groups', 'patch')), parts along dimension 0, may hold values from 0 to 512, as said below
- neighbours: int32 [16384, 32], P(('groups', 'patch')), parts along dimension 0, may hold values from 0 to 8191, as said below
- enc_grid_w: bfloat16 [512, 512], replicated, may hold values from -0.25 to 0.25
- enc_bias: float32 [512], replicated, may hold values from -4 to 4
- enc_mesh_w: bfloat16 [512, 512], replicated, may hold values from -0.25 to 0.25
- enc_msg_w: bfloat16 [512, 512], replicated, may hold values from -0.25 to 0.25
- upd_agg_w: bfloat16 [512, 512], replicated, may hold values from -0.25 to 0.25
- upd_mesh_w: bfloat16 [512, 512], replicated, may hold values from -0.25 to 0.25
- upd_out_w: bfloat16 [512, 512], replicated, may hold values from -0.25 to 0.25
- norm_gain: float32 [512], replicated, may hold values from 0.1 to 1.9
- query_w: bfloat16 [512, 512], replicated, may hold values from -0.25 to 0.25
- key_w: bfloat16 [512, 512], replicated, may hold values from -0.25 to 0.25
- value_w: bfloat16 [512, 512], replicated, may hold values from -0.25 to 0.25
- out_w: bfloat16 [512, 512], replicated, may hold values from -0.25 to 0.25
- ffn_gain: float32 [512], replicated, may hold values from 0.1 to 1.9
- ffn_in_w: bfloat16 [512, 2048], replicated, may hold values from -0.25 to 0.25
- ffn_out_w: bfloat16 [2048, 512], replicated, may hold values from -0.125 to 0.125
Outputs:
- result: bfloat16 [16384, 512], P(('groups', 'patch')), parts along dimension 0
There are 2 independent parts, one for each index of `groups`. A program takes and returns all parts, laid end to end along the dimension named above; an argument that names none is the same for every part. Nothing has to cross between parts.
Inputs may be any that keep to these rules, and one draw needn't show every extreme that they name: `enc_recv`: in each band's slots for one owner, the used edges come first and the rest hold 512; the first and last bands fill all their slots. `neighbours`: neighbour 0 of a node is the node itself; every neighbour's owner is within 2 patch indices of the node's owner, wrapping around.
All inputs are finite; a program needn't handle non-finite values.
Results may differ from a plain program's by a relative error of at most 0.006.
The roundings to bfloat16 on the way count: a program that leaves them out, or rounds other values in their place, can miss the bound.
Values may be sent and summed in bfloat16 or wider, within the bound.
A program may use at most 256 MiB of HBM per device.

v0:
```python
import math

import jax
import jax.numpy as jnp
from jax import lax
from jax.sharding import PartitionSpec as P

HEADS = 4
REACH = 2


norm_eps = 1e-05
head_eps = 1e-06


def shifted(block, axis, distance):
    devices = range(lax.axis_size(axis))
    route = [((i - distance) % len(devices), i) for i in devices]
    return lax.ppermute(block, axis, route)


def rms_scale(values, gain_vector):
    square = jnp.mean(values * values, axis=-1, keepdims=True)
    return (values * lax.rsqrt(square + norm_eps) * gain_vector).astype(jnp.bfloat16)


def scatter_rows(landing, message, row_ids):
    onehot = (row_ids[:, None] == landing[None, :]).astype(jnp.bfloat16)
    return jnp.dot(onehot, message, preferred_element_type=jnp.float32)


def pick_rows(table, row_index):
    table_ids = jnp.arange(table.shape[0], dtype=jnp.int32)
    onehot = (row_index[:, None] == table_ids[None, :]).astype(jnp.bfloat16)
    return jnp.dot(onehot, table, preferred_element_type=jnp.float32).astype(jnp.bfloat16)


def edge_message(send_rows, recv_rows, enc_msg_w):
    active = jax.nn.silu(send_rows.astype(jnp.float32) + recv_rows.astype(jnp.float32)).astype(
        jnp.bfloat16
    )
    return jnp.dot(active, enc_msg_w, preferred_element_type=jnp.float32).astype(jnp.bfloat16)


def shards(
    grid_latents,
    mesh_latents,
    enc_send,
    enc_recv,
    neighbours,
    enc_grid_w,
    enc_bias,
    enc_mesh_w,
    enc_msg_w,
    upd_agg_w,
    upd_mesh_w,
    upd_out_w,
    norm_gain,
    query_w,
    key_w,
    value_w,
    out_w,
    ffn_gain,
    ffn_in_w,
    ffn_out_w,
):
    hop_count = 2 * REACH + 1
    node_rows = mesh_latents.shape[0]
    latent_width = mesh_latents.shape[1]
    projected = (
        jnp.dot(grid_latents, enc_grid_w, preferred_element_type=jnp.float32) + enc_bias
    ).astype(jnp.bfloat16)
    receiver_proj = jnp.dot(mesh_latents, enc_mesh_w, preferred_element_type=jnp.float32).astype(
        jnp.bfloat16
    )
    senders = enc_send.reshape(hop_count, -1)
    targets = enc_recv.reshape(hop_count, -1)
    row_ids = jnp.arange(node_rows, dtype=jnp.int32)
    summed = jnp.zeros((node_rows, latent_width), jnp.float32)
    for block_slot in range(hop_count):
        offset = block_slot - REACH
        send_rows = pick_rows(projected, senders[block_slot])
        landing = targets[block_slot]
        if offset != 0:
            send_rows = shifted(send_rows, "patch", offset)
            landing = shifted(landing, "patch", offset)
        recv_rows = pick_rows(receiver_proj, jnp.minimum(landing, node_rows - 1))
        message = edge_message(send_rows, recv_rows, enc_msg_w)
        summed = summed + scatter_rows(landing, message, row_ids)
    aggregate = summed.astype(jnp.bfloat16)
    update = jax.nn.silu(
        jnp.dot(aggregate, upd_agg_w, preferred_element_type=jnp.float32)
        + jnp.dot(mesh_latents, upd_mesh_w, preferred_element_type=jnp.float32)
    ).astype(jnp.bfloat16)
    encoded = mesh_latents.astype(jnp.float32) + jnp.dot(
        update, upd_out_w, preferred_element_type=jnp.float32
    )
    normed = rms_scale(encoded, norm_gain)
    queries = jnp.dot(normed, query_w, preferred_element_type=jnp.float32).astype(jnp.bfloat16)
    pieces = []
    local_rows = jnp.concatenate(
        [
            jnp.dot(normed, key_w, preferred_element_type=jnp.float32).astype(jnp.bfloat16),
            jnp.dot(normed, value_w, preferred_element_type=jnp.float32).astype(jnp.bfloat16),
        ],
        axis=1,
    )
    for block_slot in range(hop_count):
        offset = block_slot - REACH
        if offset == 0:
            pieces.append(local_rows)
        else:
            pieces.append(shifted(local_rows, "patch", -offset))
    key_window = jnp.concatenate(pieces, axis=0)
    own_index = lax.axis_index("patch")
    device_count = lax.axis_size("patch")
    owners = neighbours // node_rows
    position = (owners - own_index + REACH) % device_count * node_rows + neighbours % node_rows
    head_size = latent_width // HEADS
    window_rows = key_window.shape[0]
    window_keys = key_window[:, :latent_width].reshape(window_rows, HEADS, head_size)
    window_values = (
        key_window[:, latent_width:].reshape(window_rows, HEADS, head_size).astype(jnp.float32)
    )
    query_per_head = queries.reshape(node_rows, HEADS, head_size)
    all_products = jnp.einsum(
        "nhd,jhd->njh", query_per_head, window_keys, preferred_element_type=jnp.float32
    )
    window_squares = jnp.einsum(
        "jhd,jhd->jh", window_keys, window_keys, preferred_element_type=jnp.float32
    )
    window_ids = jnp.arange(window_rows, dtype=jnp.int32)
    selector = (position[:, :, None] == window_ids[None, None, :]).astype(jnp.float32)
    score_products = jnp.einsum(
        "nkj,njh->nkh", selector, all_products, precision=lax.Precision.HIGHEST
    )
    key_sq = jnp.einsum("nkj,jh->nkh", selector, window_squares, precision=lax.Precision.HIGHEST)
    query_squares = jnp.einsum(
        "tfe,tfe->tf", query_per_head, query_per_head, preferred_element_type=jnp.float32
    )
    scores = (
        score_products
        * lax.rsqrt(query_squares / head_size + head_eps)[:, None, :]
        * lax.rsqrt(key_sq / head_size + head_eps)
        / math.sqrt(head_size)
    )
    exponent = jnp.exp(scores)
    attention_weights = (exponent / jnp.sum(exponent, axis=1, keepdims=True)).astype(jnp.bfloat16)
    folded = jnp.einsum(
        "nkh,nkj->njh",
        attention_weights.astype(jnp.float32),
        selector,
        precision=lax.Precision.HIGHEST,
    )
    attention_mixture = jnp.einsum(
        "njh,jhd->nhd", folded, window_values, precision=lax.Precision.HIGHEST
    )
    attended = attention_mixture.astype(jnp.bfloat16).reshape(node_rows, latent_width)
    hidden = encoded + jnp.dot(attended, out_w, preferred_element_type=jnp.float32)
    normed_ffn = rms_scale(hidden, ffn_gain)
    expanded = jax.nn.silu(
        jnp.dot(normed_ffn, ffn_in_w, preferred_element_type=jnp.float32)
    ).astype(jnp.bfloat16)
    return (hidden + jnp.dot(expanded, ffn_out_w, preferred_element_type=jnp.float32)).astype(
        jnp.bfloat16
    )


def solution(mesh):
    in_specs = (
        P(("groups", "patch"), None),
        P(("groups", "patch"), None),
        P(("groups", "patch"), None),
        P(("groups", "patch"), None),
        P(("groups", "patch"), None),
        P(),
        P(),
        P(),
        P(),
        P(),
        P(),
        P(),
        P(),
        P(),
        P(),
        P(),
        P(),
        P(),
        P(),
        P(),
    )
    out_specs = P(("groups", "patch"), None)
    return jax.shard_map(shards, mesh=mesh, in_specs=in_specs, out_specs=out_specs, check_vma=False)
```

profile of v0, /device:TPU:1, one launch (start us, length us, event | category | flops | bytes accessed | tf_op | source)
XLA Modules:
  0.0 637.1 jit_solution(5124580415649901565)
XLA Ops:
  0.9 2.6 collective-permute-start.4
  3.5 3.2 collective-permute-start
  11.1 4.2 collective-permute-start.1
  16.0 2.9 fusion.20
  18.9 2.8 fusion.21
  26.9 3.0 fusion.36
  33.9 22.8 %collective-permute-done.3 = bf16[512,512]{1,0:T(8,128)(2,1)S(1)} collective-permute-done((bf16[512,512]{1,0:T(8,128)(2,1)}, bf16[512,512]{1,0:T(8,128)(2,1)S(1)}, u32[]{:S(2)}, u32[]{:S(2)}) %collective-permute-start.3) | collective-permute-done | bytes 524320 | tf_op jit(solution)/shard_map/ppermute | solution.py:19
  59.6 2.8 fusion.35
  62.4 2.8 fusion.37
  67.7 2.7 convolution_convert_fusion.5
  70.4 2.6 fusion.16
  73.1 3.2 fusion.38
  76.3 2.8 multiply_reduce_fusion.1
  86.8 29.1 %iota_compare_fusion = pred[512,32,2560]{2,0,1:T(32,128)(4,1)} fusion(s32[512,32]{0,1:T(8,128)S(1)} %fusion.73), kind=kLoop, calls=%fused_computation | loop fusion | flops 41943040 | bytes 42008576 | tf_op jit(solution)/shard_map/eq | solution.py:133
  116.4 31.8 %collective-permute-done.8 = bf16[512,1024]{0,1:T(8,128)(2,1)S(1)} collective-permute-done((bf16[512,1024]{0,1:T(8,128)(2,1)S(1)}, bf16[512,1024]{0,1:T(8,128)(2,1)S(1)}, u32[]{:S(2)}, u32[]{:S(2)}) %collective-permute-start.8) | collective-permute-done | bytes 1048608 | tf_op jit(solution)/shard_map/ppermute | solution.py:19
  148.5 2.8 collective-permute-done.10
  153.9 78.6 %fusion.8 = f32[512,32,4]{0,2,1:T(4,128)} fusion(s32[512,32]{0,1:T(8,128)S(1)} %fusion.73, f32[2560,4]{0,1:T(4,128)S(1)} %fusion.7), kind=kOutput, calls=%fused_computation.10 | convolution fusion | flops 2055208960 | bytes 368640 | tf_op jit(solution)/shard_map/nkj,jh->nkh/dot_general | solution.py:137
  232.5 8.5 %fusion.81 = f32[4,2560,512]{2,1,0:T(8,128)} fusion(bf16[2560,4,128]{0,2,1:T(8,128)(2,1)S(1)} %bitcast.79, bf16[512,4,128]{0,2,1:T(8,128)(2,1)S(1)} %bitcast.81), kind=kOutput, calls=%fused_computation.159 | convolution fusion | flops 1342177280 | bytes 24117248 | tf_op jit(solution)/shard_map/nhd,jhd->njh/dot_general | solution.py:126
  241.1 25.1 %copy.32 = f32[4,2560,512]{1,0,2:T(4,128)} copy(f32[4,2560,512]{2,1,0:T(8,128)} %fusion.81) | data formatting | bytes 41943040 | tf_op jit(solution)/shard_map/nhd,jhd->njh/dot_general | solution.py:126
  266.2 199.7 %fusion.2 = f32[512,32,4]{1,2,0:T(4,128)S(1)} fusion(pred[512,32,2560]{2,0,1:T(32,128)(4,1)} %iota_compare_fusion, f32[4,2560,512]{1,0,2:T(4,128)} %copy.32), kind=kOutput, calls=%fused_computation.3 | convolution fusion | flops 2013265920 | bytes 63176704 | tf_op jit(solution)/shard_map/nkj,njh->nkh/dot_general | solution.py:134
  468.8 142.3 %fusion = f32[512,2560,4]{1,2,0:T(4,128)} fusion(bf16[512,32,4]{1,2,0:T(4,128)(2,1)S(1)} %copy.39, pred[512,32,2560]{2,0,1:T(32,128)(4,1)} %iota_compare_fusion), kind=kOutput, calls=%fused_computation.1 | convolution fusion | flops 335544320 | bytes 63045632 | tf_op jit(solution)/shard_map/nkh,nkj->njh/dot_general | solution.py:149
  611.1 17.0 %fusion.32 = bf16[4,128,512]{2,1,0:T(8,128)(2,1)S(1)} fusion(bf16[2560,4,128]{0,2,1:T(8,128)(2,1)} %bitcast.78, f32[512,2560,4]{1,2,0:T(4,128)} %fusion), kind=kOutput, calls=%fused_computation.60 | convolution fusion | flops 8053325824 | bytes 24117248 | tf_op jit(solution)/shard_map/njh,jhd->nhd/dot_general | solution.py:155
  628.1 2.7 multiply_reduce_fusion
  630.8 5.0 fusion.18
  (78 shorter events, 35.4 us)
Async XLA Ops:
  0.0 630.8 %copy-start = (bf16[2048,512]{1,0:T(8,128)(2,1)S(1)}, bf16[2048,512]{1,0:T(8,128)(2,1)}, u32[]{:S(2)}) copy-start(bf16[2048,512]{1,0:T(8,128)(2,1)} %param.39) | copy-start | bytes 6291460
  0.9 30.1 %collective-permute-start.4 = (s32[512]{0:T(512)S(1)}, s32[512]{0:T(512)S(1)}, u32[]{:S(2)}, u32[]{:S(2)}) collective-permute-start(s32[512]{0:T(512)S(1)} %get-tuple-element.7), channel_id=1, source_target_pairs={{15,0},{0,1},{1,2},{2,3},{3,4},{4,5},{5,6},{6,7},{7,8},{8,9},{9,10... | collective-permute-start | bytes 6152 | tf_op jit(solution)/shard_map/ppermute | solution.py:19
  3.5 30.0 %collective-permute-start.2 = (s32[512]{0:T(512)S(1)}, s32[512]{0:T(512)S(1)}, u32[]{:S(2)}, u32[]{:S(2)}) collective-permute-start(s32[512]{0:T(512)S(1)} %get-tuple-element.9), channel_id=1, source_target_pairs={{1,0},{2,1},{3,2},{4,3},{5,4},{6,5},{7,6},{8,7},{9,8},{10,9},{11,1... | collective-permute-start | bytes 6152 | tf_op jit(solution)/shard_map/ppermute | solution.py:19
  3.5 30.0 %collective-permute-start = (s32[512]{0:T(512)S(1)}, s32[512]{0:T(512)S(1)}, u32[]{:S(2)}, u32[]{:S(2)}) collective-permute-start(s32[512]{0:T(512)S(1)} %get-tuple-element.10), channel_id=1, source_target_pairs={{2,0},{3,1},{4,2},{5,3},{6,4},{7,5},{8,6},{9,7},{10,8},{11,9},{12,... | collective-permute-start | bytes 6152 | tf_op jit(solution)/shard_map/ppermute | solution.py:19
  6.7 27.1 %collective-permute-start.6 = (s32[512]{0:T(512)S(1)}, s32[512]{0:T(512)S(1)}, u32[]{:S(2)}, u32[]{:S(2)}) collective-permute-start(s32[512]{0:T(512)S(1)} %get-tuple-element.11), channel_id=1, source_target_pairs={{14,0},{15,1},{0,2},{1,3},{2,4},{3,5},{4,6},{5,7},{6,8},{7,9},{8,1... | collective-permute-start | bytes 6152 | tf_op jit(solution)/shard_map/ppermute | solution.py:19
  9.6 5.7 copy-start.9
  11.1 12.1 %copy-start.2 = (bf16[512,512]{1,0:T(8,128)(2,1)S(1)}, bf16[512,512]{1,0:T(8,128)(2,1)}, u32[]{:S(2)}) copy-start(bf16[512,512]{1,0:T(8,128)(2,1)} %param.21) | copy-start | bytes 1572868
  11.1 54.0 %collective-permute-start.1 = (bf16[512,512]{1,0:T(8,128)(2,1)}, bf16[512,512]{1,0:T(8,128)(2,1)}, u32[]{:S(2)}, u32[]{:S(2)}) collective-permute-start(bf16[512,512]{1,0:T(8,128)(2,1)} %fusion.26), channel_id=1, source_target_pairs={{2,0},{3,1},{4,2},{5,3},{6,4},{7,5},{8,6},{9,7},{10,8},{11,9},{12,... | collective-permute-start | bytes 1572872 | tf_op jit(solution)/shard_map/ppermute | solution.py:19
  16.0 5.6 copy-start.10
  25.2 4.7 copy-start.5
  31.0 25.7 %collective-permute-start.3 = (bf16[512,512]{1,0:T(8,128)(2,1)}, bf16[512,512]{1,0:T(8,128)(2,1)S(1)}, u32[]{:S(2)}, u32[]{:S(2)}) collective-permute-start(bf16[512,512]{1,0:T(8,128)(2,1)} %fusion.25), channel_id=1, source_target_pairs={{1,0},{2,1},{3,2},{4,3},{5,4},{6,5},{7,6},{8,7},{9,8},{10,9},{11,1... | collective-permute-start | bytes 1572872 | tf_op jit(solution)/shard_map/ppermute | solution.py:19
  33.6 34.1 %collective-permute-start.5 = (bf16[512,512]{1,0:T(8,128)(2,1)}, bf16[512,512]{1,0:T(8,128)(2,1)}, u32[]{:S(2)}, u32[]{:S(2)}) collective-permute-start(bf16[512,512]{1,0:T(8,128)(2,1)} %fusion.21), channel_id=1, source_target_pairs={{15,0},{0,1},{1,2},{2,3},{3,4},{4,5},{5,6},{6,7},{7,8},{8,9},{9,10... | collective-permute-start | bytes 1572872 | tf_op jit(solution)/shard_map/ppermute | solution.py:19
  33.6 24.6 %collective-permute-start.7 = (bf16[512,512]{1,0:T(8,128)(2,1)}, bf16[512,512]{1,0:T(8,128)(2,1)S(1)}, u32[]{:S(2)}, u32[]{:S(2)}) collective-permute-start(bf16[512,512]{1,0:T(8,128)(2,1)} %fusion.20), channel_id=1, source_target_pairs={{14,0},{15,1},{0,2},{1,3},{2,4},{3,5},{4,6},{5,7},{6,8},{7,9},{8,1... | collective-permute-start | bytes 1572872 | tf_op jit(solution)/shard_map/ppermute | solution.py:19
  33.9 25.7 %copy-start.4 = (bf16[512,512]{1,0:T(8,128)(2,1)S(1)}, bf16[512,512]{1,0:T(8,128)(2,1)}, u32[]{:S(2)}) copy-start(bf16[512,512]{1,0:T(8,128)(2,1)} %param.28) | copy-start | bytes 1572868
  73.0 6.1 copy-start.6
  79.1 36.8 %copy-start.1 = (f32[512,512]{0,1:T(8,128)}, f32[512,512]{0,1:T(8,128)S(1)}, u32[]{:S(2)}) copy-start(f32[512,512]{0,1:T(8,128)S(1)} %get-tuple-element.18) | copy-start | bytes 3145732
  82.7 33.3 %copy-start.7 = (bf16[512,512]{1,0:T(8,128)(2,1)S(1)}, bf16[512,512]{1,0:T(8,128)(2,1)}, u32[]{:S(2)}) copy-start(bf16[512,512]{1,0:T(8,128)(2,1)} %param.33) | copy-start | bytes 1572868
  82.7 68.7 %collective-permute-start.11 = (bf16[512,1024]{0,1:T(8,128)(2,1)S(1)}, bf16[512,1024]{0,1:T(8,128)(2,1)S(1)}, u32[]{:S(2)}, u32[]{:S(2)}) collective-permute-start(bf16[512,1024]{0,1:T(8,128)(2,1)S(1)} %pad_maximum_fusion), channel_id=1, source_target_pairs={{2,0},{3,1},{4,2},{5,3},{6,4},{7,5},{8,6},{9,7},{10,8},{11,9},{12,... | collective-permute-start | bytes 3145736 | tf_op jit(solution)/shard_map/ppermute | solution.py:19
  82.9 68.4 %collective-permute-start.10 = (bf16[512,1024]{0,1:T(8,128)(2,1)S(1)}, bf16[512,1024]{0,1:T(8,128)(2,1)S(1)}, u32[]{:S(2)}, u32[]{:S(2)}) collective-permute-start(bf16[512,1024]{0,1:T(8,128)(2,1)S(1)} %pad_maximum_fusion), channel_id=1, source_target_pairs={{1,0},{2,1},{3,2},{4,3},{5,4},{6,5},{7,6},{8,7},{9,8},{10,9},{11,1... | collective-permute-start | bytes 3145736 | tf_op jit(solution)/shard_map/ppermute | solution.py:19
  83.5 64.8 %collective-permute-start.9 = (bf16[512,1024]{0,1:T(8,128)(2,1)S(1)}, bf16[512,1024]{0,1:T(8,128)(2,1)S(1)}, u32[]{:S(2)}, u32[]{:S(2)}) collective-permute-start(bf16[512,1024]{0,1:T(8,128)(2,1)S(1)} %pad_maximum_fusion), channel_id=1, source_target_pairs={{15,0},{0,1},{1,2},{2,3},{3,4},{4,5},{5,6},{6,7},{7,8},{8,9},{9,10... | collective-permute-start | bytes 3145736 | tf_op jit(solution)/shard_map/ppermute | solution.py:19
  84.7 63.6 %collective-permute-start.8 = (bf16[512,1024]{0,1:T(8,128)(2,1)S(1)}, bf16[512,1024]{0,1:T(8,128)(2,1)S(1)}, u32[]{:S(2)}, u32[]{:S(2)}) collective-permute-start(bf16[512,1024]{0,1:T(8,128)(2,1)S(1)} %pad_maximum_fusion), channel_id=1, source_target_pairs={{14,0},{15,1},{0,2},{1,3},{2,4},{3,5},{4,6},{5,7},{6,8},{7,9},{8,1... | collective-permute-start | bytes 3145736 | tf_op jit(solution)/shard_map/ppermute | solution.py:19
  611.0 17.1 %copy-start.3 = (bf16[512,512]{1,0:T(8,128)(2,1)S(1)}, bf16[512,512]{1,0:T(8,128)(2,1)}, u32[]{:S(2)}) copy-start(bf16[512,512]{1,0:T(8,128)(2,1)} %param.36) | copy-start | bytes 1572868
  611.0 19.8 %copy-start.8 = (f32[512]{0:T(512)S(1)}, f32[512]{0:T(512)}, u32[]{:S(2)}) copy-start(f32[512]{0:T(512)} %param.37) | copy-start | bytes 6148
where the time goes:
time: 643 us; the launch traced here: 637 us
  matrix products  498 us (77%)
  waiting for transfers between devices  57.5 us (9%)
  other arithmetic  33 us (5%)
  local copies, waits for them, and re-layouts  31.7 us (5%)
  starting transfers between devices  16.9 us (3%)
    dot_general x1, matrix products, shards(): jnp.einsum('nkj,njh->nkh', selector, all_products, precision=lax.Precisio...  200 us
    dot_general x1, matrix products, shards(): jnp.einsum('nkh,nkj->njh', attention_weights.astype(jnp.float32), selecto...  142 us
    dot_general x1, matrix products, shards(): jnp.einsum('nkj,jh->nkh', selector, window_squares, precision=lax.Precisi...  78.6 us
    ppermute x12, waiting for transfers between devices, shifted(): return lax.ppermute(block, axis, route)  57.5 us
    eq x1, other arithmetic, shards(): position[:, :, None] == window_ids[None, None, :]  29.1 us
    dot_general x1, local copies, waits for them, and re-layouts, shards(): jnp.einsum('nhd,jhd->njh', query_per_head, window_keys, preferred_element...  25.1 us
    dot_general x1, matrix products, shards(): jnp.einsum('njh,jhd->nhd', folded, window_values, precision=lax.Precision...  17 us
    ppermute x12, starting transfers between devices, shifted(): return lax.ppermute(block, axis, route)  16.9 us
  transfers between devices with their start and end apart: 12, of which 3 were waited for; matrix products, arithmetic and copies ran while one was open for 10% of the time, Pallas kernels for 0%

commit v1 on v0

v1 whole, which is shorter than its diff:
```python
import functools
import math

import jax
import jax.numpy as jnp
from jax import lax
from jax.experimental import pallas as pl
from jax.experimental.pallas import tpu as pltpu
from jax.sharding import PartitionSpec as P

HEADS = 4
REACH = 2
SLOTS = 2 * REACH + 1
LANES = 128
GROUP = 8
CHUNKS = 4

norm_eps = 1e-05
head_eps = 1e-06
BF = jnp.bfloat16
F32 = jnp.float32


def dot(a, b):
    return jnp.dot(a, b, preferred_element_type=F32)


def dot_nt(a, b):
    return lax.dot_general(a, b, (((1,), (1,)), ((), ())), preferred_element_type=F32)


def silu(v):
    return v / (1.0 + jnp.exp(-v))


def rms_scale(values, gain):
    square = jnp.mean(values * values, axis=-1, keepdims=True)
    return (values * lax.rsqrt(square + norm_eps) * gain).astype(BF)


def exchange_body(count, parts, *refs):
    arrays = len(parts)
    srcs, wins = refs[:arrays], refs[arrays : 2 * arrays]
    send, recv, local = refs[2 * arrays :]
    me = lax.axis_index("patch")
    core = me % 2
    chip_odd = (me // 2) % 2
    partner = me + 1 - 2 * core
    mate = me + 2 - 4 * chip_odd
    far = (me + 4 - 8 * chip_odd + count) % count
    far_from = (me - 4 + 8 * chip_odd + count) % count
    mate_slot = 4 - 4 * chip_odd
    far_slot = 4 * chip_odd

    barrier = pltpu.get_barrier_semaphore()
    for other in (partner, mate, far, far_from):
        pl.semaphore_signal(
            barrier, inc=1, device_id={"patch": other}, device_id_type=pl.DeviceIdType.MESH
        )
    pl.semaphore_wait(barrier, 4)

    def remote(src, dst, sem, other):
        return pltpu.make_async_remote_copy(
            src_ref=src,
            dst_ref=dst,
            send_sem=send.at[sem],
            recv_sem=recv.at[sem],
            device_id={"patch": other},
            device_id_type=pl.DeviceIdType.MESH,
        )

    pieces = []
    for a in range(arrays):
        rows = srcs[a].shape[0] // parts[a]
        for c in range(parts[a]):
            pieces.append((a, c * rows, rows))
    total = len(pieces)
    to_mate, to_partner, onward, passed, own = [], [], [], [], []
    for i, (a, r, n) in enumerate(pieces):
        copy = remote(srcs[a].at[pl.ds(r, n)], wins[a].at[far_slot, pl.ds(r, n)], i, mate)
        copy.start()
        to_mate.append(copy)
    for i, (a, r, n) in enumerate(pieces):
        copy = remote(
            srcs[a].at[pl.ds(r, n)], wins[a].at[1 + 2 * core, pl.ds(r, n)], total + i, partner
        )
        copy.start()
        to_partner.append(copy)
    for a in range(arrays):
        copy = pltpu.make_async_copy(srcs[a], wins[a].at[REACH], local.at[a])
        copy.start()
        own.append(copy)
    for i, (a, r, n) in enumerate(pieces):
        to_mate[i].wait_recv()
        copy = remote(
            wins[a].at[mate_slot, pl.ds(r, n)],
            wins[a].at[far_slot, pl.ds(r, n)],
            2 * total + i,
            far,
        )
        copy.start()
        onward.append(copy)
    for i, (a, r, n) in enumerate(pieces):
        onward[i].wait_recv()
        copy = remote(
            wins[a].at[4 - 4 * core, pl.ds(r, n)],
            wins[a].at[3 - 2 * core, pl.ds(r, n)],
            3 * total + i,
            partner,
        )
        copy.start()
        passed.append(copy)
    for copy in to_partner + passed:
        copy.wait_recv()
    for copy in to_mate + to_partner + onward + passed:
        copy.wait_send()
    for copy in own:
        copy.wait()


def exchange(count, collective_id, parts, *arrays):
    total = sum(parts)
    vmem = pl.BlockSpec(memory_space=pltpu.VMEM)
    return pl.pallas_call(
        functools.partial(exchange_body, count, parts),
        out_shape=[jax.ShapeDtypeStruct((SLOTS,) + a.shape, a.dtype) for a in arrays],
        in_specs=[vmem] * len(arrays),
        out_specs=[vmem] * len(arrays),
        scratch_shapes=[
            pltpu.SemaphoreType.DMA((4 * total,)),
            pltpu.SemaphoreType.DMA((4 * total,)),
            pltpu.SemaphoreType.DMA((len(arrays),)),
        ],
        compiler_params=pltpu.CompilerParams(collective_id=collective_id, has_side_effects=True),
        name="exchange",
    )(*arrays)


def encode_body(
    window, send_col, recv_col, recv_row, mesh, grid_w, bias, mesh_w, msg_w, agg_w, upd_w, out_w,
    gain, encoded_ref, normed_ref, table,
):
    grid_rows = window.shape[1]
    nodes = mesh.shape[0]
    edges = send_col.shape[1]
    half = edges // 2
    table[grid_rows:, :] = dot(mesh[...], mesh_w[...]).astype(BF)

    def hop(slot, summed):
        table[:grid_rows, :] = (dot(window[slot], grid_w[...]) + bias[...]).astype(BF)
        messages = []
        for e in (0, half):
            s = send_col[slot, pl.ds(e, half)]
            r = jnp.minimum(recv_col[slot, pl.ds(e, half)], nodes - 1)
            lane_g = lax.broadcasted_iota(jnp.int32, (half, grid_rows), 1)
            lane_m = lax.broadcasted_iota(jnp.int32, (half, nodes), 1)
            pick_s = jnp.where(s == lane_g, 1.0, 0.0).astype(BF)
            pick_r = jnp.where(r == lane_m, 1.0, 0.0).astype(BF)
            both = dot(pick_s, table[:grid_rows, :]) + dot(pick_r, table[grid_rows:, :])
            messages.append(dot(silu(both).astype(BF), msg_w[...]).astype(BF))
        message = jnp.concatenate(messages, axis=0)
        row = lax.broadcasted_iota(jnp.int32, (nodes, edges), 0)
        spread = jnp.where(recv_row[slot] == row, 1.0, 0.0).astype(BF)
        return summed + dot(spread, message)

    summed = lax.fori_loop(0, SLOTS, hop, jnp.zeros(mesh.shape, F32))
    aggregate = summed.astype(BF)
    update = silu(dot(aggregate, agg_w[...]) + dot(mesh[...], upd_w[...])).astype(BF)
    encoded = mesh[...].astype(F32) + dot(update, out_w[...])
    encoded_ref[...] = encoded
    normed_ref[...] = rms_scale(encoded, gain[...])


def attend_body(
    window, encoded, code, low, query_w, key_w, value_w, out_w, gain, in_w, ffn_w, result,
    counts, queries, keys, values, key_scale, attended,
):
    nodes, width = encoded.shape
    head = width // HEADS
    span = SLOTS * nodes
    tiles = span // LANES
    for slot in range(SLOTS):
        rows = pl.ds(slot * nodes, nodes)
        block = window[slot]
        keys[rows, :] = dot(block, key_w[...]).astype(BF)
        values[rows, :] = dot(block, value_w[...]).astype(BF)
    queries[...] = dot(window[REACH], query_w[...]).astype(BF)

    def count_group(g, carry):
        packed = GROUP * LANES // code.shape[2]
        left_row = lax.broadcasted_iota(jnp.int32, (tiles * GROUP, code.shape[2]), 0)
        right_row = lax.broadcasted_iota(jnp.int32, (LANES, code.shape[2]), 0)
        left = jnp.where(code[g] == left_row, 1.0, 0.0).astype(BF)
        right = jnp.where(low[g] == right_row, 1.0, 0.0).astype(BF)
        found = dot_nt(left, right)
        rows = pl.ds(pl.multiple_of(g * GROUP, GROUP), GROUP)
        for t in range(tiles):
            counts[rows, t * LANES : (t + 1) * LANES] = found[t * GROUP : (t + 1) * GROUP, :]
        return carry

    lax.fori_loop(0, nodes // GROUP, count_group, 0, unroll=2)

    for slot in range(SLOTS):
        cols = slice(slot * nodes, (slot + 1) * nodes)
        k = keys[cols, :].astype(F32)
        square = k * k
        upper = square.astype(BF)
        lower = (square - upper.astype(F32)).astype(BF)
        pick_row = lax.broadcasted_iota(jnp.int32, (GROUP, width), 0)
        pick_lane = lax.broadcasted_iota(jnp.int32, (GROUP, width), 1)
        pick = jnp.where(pick_lane // head == pick_row, 1.0, 0.0).astype(BF)
        sums = dot_nt(pick, upper) + dot_nt(pick, lower)
        key_scale[:, cols] = lax.rsqrt(sums / head + head_eps)

    tile = LANES

    def attend_tile(t, carry):
        rows = pl.ds(pl.multiple_of(t * tile, tile), tile)
        for h in range(HEADS):
            cols = slice(h * head, (h + 1) * head)
            q = queries[rows, cols]
            qf = q.astype(F32)
            q_scale = lax.rsqrt(jnp.sum(qf * qf, axis=1, keepdims=True) / head + head_eps)
            q_scale = q_scale * (1.0 / math.sqrt(head))
            scores = dot_nt(q, keys[:, cols]) * q_scale * key_scale[h : h + 1, :]
            exponent = jnp.exp(scores)
            c = counts[rows, :]
            inverse = 1.0 / jnp.sum(exponent * c, axis=1, keepdims=True)
            weight = (exponent * inverse).astype(BF).astype(F32)
            mixed = dot((weight * c).astype(BF), values[:, cols])
            attended[rows, cols] = mixed.astype(BF)
        return carry

    lax.fori_loop(0, nodes // tile, attend_tile, 0)

    hidden = encoded[...] + dot(attended[...], out_w[...])
    normed = rms_scale(hidden, gain[...])
    wide = in_w.shape[1]
    step = wide // 4
    total = hidden
    for f in range(0, wide, step):
        expanded = silu(dot(normed, in_w[:, f : f + step])).astype(BF)
        total = total + dot(expanded, ffn_w[f : f + step, :])
    result[...] = total.astype(BF)


def shards(
    grid_latents, mesh_latents, enc_send, enc_recv, neighbours, enc_grid_w, enc_bias, enc_mesh_w,
    enc_msg_w, upd_agg_w, upd_mesh_w, upd_out_w, norm_gain, query_w, key_w, value_w, out_w,
    ffn_gain, ffn_in_w, ffn_out_w,
):
    count = lax.axis_size("patch")
    nodes, width = mesh_latents.shape
    own_index = lax.axis_index("patch")
    blocks = enc_send.shape[0] // SLOTS
    edges = blocks * enc_send.shape[1]
    vmem = pl.BlockSpec(memory_space=pltpu.VMEM)
    params = pltpu.CompilerParams(vmem_limit_bytes=60 * 1024 * 1024)

    ends = jnp.concatenate([enc_send.reshape(SLOTS, edges), enc_recv.reshape(SLOTS, edges)], axis=0)
    ends = jnp.pad(ends, ((0, 16 - 2 * SLOTS), (0, 0)))
    grid_window, end_window = exchange(count, 0, (CHUNKS, 1), grid_latents, ends)
    sends = jnp.stack([end_window[s, SLOTS - 1 - s] for s in range(SLOTS)])
    recvs = jnp.stack([end_window[s, 2 * SLOTS - 1 - s] for s in range(SLOTS)])

    encoded, normed = pl.pallas_call(
        encode_body,
        out_shape=[
            jax.ShapeDtypeStruct((nodes, width), F32),
            jax.ShapeDtypeStruct((nodes, width), BF),
        ],
        in_specs=[vmem] * 13,
        out_specs=[vmem] * 2,
        scratch_shapes=[pltpu.VMEM((grid_latents.shape[0] + nodes, width), BF)],
        compiler_params=params,
        name="encode",
    )(
        grid_window, sends[:, :, None], recvs[:, :, None], recvs[:, None, :], mesh_latents,
        enc_grid_w, enc_bias[None, :], enc_mesh_w, enc_msg_w, upd_agg_w, upd_mesh_w, upd_out_w,
        norm_gain[None, :],
    )

    (window,) = exchange(count, 1, (CHUNKS,), normed)

    owners = neighbours // nodes
    position = (owners - own_index + REACH) % count * nodes + neighbours % nodes
    lane = jnp.arange(nodes, dtype=jnp.int32)[:, None] % GROUP
    packed = (nodes // GROUP, 1, GROUP * neighbours.shape[1])
    code = (position // LANES * GROUP + lane).reshape(packed)
    low = (position % LANES).reshape(packed)
    return pl.pallas_call(
        attend_body,
        out_shape=jax.ShapeDtypeStruct((nodes, width), BF),
        in_specs=[vmem] * 11,
        out_specs=vmem,
        scratch_shapes=[
            pltpu.VMEM((nodes, SLOTS * nodes), F32),
            pltpu.VMEM((nodes, width), BF),
            pltpu.VMEM((SLOTS * nodes, width), BF),
            pltpu.VMEM((SLOTS * nodes, width), BF),
            pltpu.VMEM((GROUP, SLOTS * nodes), F32),
            pltpu.VMEM((nodes, width), BF),
        ],
        compiler_params=params,
        name="attend",
    )(
        window, encoded, code, low, query_w, key_w, value_w, out_w, ffn_gain[None, :], ffn_in_w,
        ffn_out_w,
    )


def solution(mesh):
    rows = P(("groups", "patch"), None)
    in_specs = (rows,) * 5 + (P(),) * 15
    return jax.shard_map(shards, mesh=mesh, in_specs=in_specs, out_specs=rows, check_vma=False)
```

time: 643 us -> 126 us (0.20)
  matrix products: 498 us -> 0 us
  Pallas kernels: 0 us -> 116 us
  waiting for transfers between devices: 57.5 us -> 0 us
  other arithmetic: 33 us -> 0.19 us
  local copies, waits for them, and re-layouts: 31.7 us -> 8.47 us
  starting transfers between devices: 16.9 us -> 0 us
    dot_general x28 -> x0, matrix products: 498 us -> none  [the longest x1 200 us: shards(): jnp.einsum('nkj,njh->nkh', selector, all_products, precision=lax.Precisio...]
    pallas_call x0 -> x4, Pallas kernels: none -> 116 us  [the longest x2 64.7 us: exchange(): pl.pallas_call(functools.partial(exchange_body, count, parts), out_shape=...]
    ppermute x12 -> x0, waiting for transfers between devices: 57.5 us -> none  [shifted(): return lax.ppermute(block, axis, route)]
    eq x1 -> x0, other arithmetic: 29.1 us -> none  [shards(): position[:, :, None] == window_ids[None, None, :]]
    dot_general x2 -> x0, local copies, waits for them, and re-layouts: 25.4 us -> none  [the longest x1 25.1 us: shards(): jnp.einsum('nhd,jhd->njh', query_per_head, window_keys, preferred_element...]
    ppermute x12 -> x0, starting transfers between devices: 16.9 us -> none  [shifted(): return lax.ppermute(block, axis, route)]
  transfers between devices with their start and end apart: 12 -> 0, of which waited for: 3 -> 0; matrix products, arithmetic and copies ran while one was open for 10% -> 0% of each run, Pallas kernels for 0% -> 0%
where the time goes in v1:
time: 126 us; the launch traced here: 125 us
  Pallas kernels  116 us (92%)
  local copies, waits for them, and re-layouts  8.47 us (7%)
    pallas_call x2, Pallas kernels, exchange(): pl.pallas_call(functools.partial(exchange_body, count, parts), out_shape=...  64.7 us
    pallas_call x1, Pallas kernels, shards(): pl.pallas_call(attend_body, out_shape=jax.ShapeDtypeStruct((nodes, width)...  32.3 us
    pallas_call x1, Pallas kernels, shards(): pl.pallas_call(encode_body, out_shape=[jax.ShapeDtypeStruct((nodes, width...  19.5 us

profile of v1, /device:TPU:1, one launch (start us, length us, event | category | flops | bytes accessed | tf_op | source)
XLA Modules:
  0.0 125.2 jit_solution(4907331144742770524)
XLA Ops:
  0.0 0.7 reshape.27
  0.7 0.7 reshape.28
  1.4 0.6 pad.4.refs_1_
  2.1 41.7 %exchange.2 = (bf16[5,1024,512]{2,1,0:T(8,128)(2,1)}, s32[5,16,512]{2,1,0:T(8,128)}) custom-call(bf16[1024,512]{1,0:T(8,128)(2,1)} %refs_0_.1, s32[16,512]{1,0:T(8,128)} %pad.4.refs_1_), custom_call_target="tpu_custom_call" | custom-call | tf_op jit(solution)/shard_map/exchange/pallas_call | solution.py:124
  43.8 0.9 slice_bitcast_fusion
  44.7 1.5 %copy.25.recv_col = s32[5,512,1]{2,1,0:T(8,128)} copy(s32[5,512,1]{1,0,2:T(8,128)S(1)} %bitcast.25) | data formatting | bytes 20480 | tf_op jit(solution)/shard_map/broadcast_in_dim | solution.py:278
  46.2 0.6 broadcast_in_dim.21.recv_row
  46.9 1.6 %copy.24.send_col = s32[5,512,1]{2,1,0:T(8,128)} copy(s32[5,512,1]{1,0,2:T(8,128)S(1)} %bitcast.26) | data formatting | bytes 20480 | tf_op jit(solution)/shard_map/broadcast_in_dim | solution.py:278
  48.4 19.5 %encode.1 = (f32[512,512]{1,0:T(8,128)}, bf16[512,512]{1,0:T(8,128)(2,1)}) custom-call(bf16[5,1024,512]{2,1,0:T(8,128)(2,1)} %get-tuple-element.9.window, s32[5,512,1]{2,1,0:T(8,128)} %copy.24.send_col, s32[5,512,1]{2,1,0:T(8,128)} %copy.25.recv_col, s32[5,1,512]{2,1,0:T(1,128)} %broadcast_in_dim.21.recv_row, bf16[512,512]{1,0:T(8,128)(2,1)} %mesh.1, ...), custom_call_target="tpu_custom_call" | custom-call | tf_op jit(solution)/shard_map/encode/pallas_call | solution.py:266
  67.9 0.0 copy-start
  67.9 22.9 %exchange.3.window = bf16[5,512,512]{2,1,0:T(8,128)(2,1)} custom-call(bf16[512,512]{1,0:T(8,128)(2,1)} %get-tuple-element.11.refs_0_), custom_call_target="tpu_custom_call" | custom-call | tf_op jit(solution)/shard_map/exchange/pallas_call | solution.py:124
  90.8 0.0 copy-done
  90.8 0.1 add_select_fusion
  91.0 0.1 copy.26
  91.2 0.8 reshape.31.code
  92.0 0.1 copy.27
  92.1 0.8 reshape.32.low
  92.9 32.3 %attend.1 = bf16[512,512]{1,0:T(8,128)(2,1)} custom-call(bf16[5,512,512]{2,1,0:T(8,128)(2,1)} %exchange.3.window, f32[512,512]{1,0:T(8,128)} %get-tuple-element.12.encoded, s32[64,1,256]{2,1,0:T(1,128)} %reshape.31.code, s32[64,1,256]{2,1,0:T(1,128)} %reshape.32.low, bf16[512,512]{1,0:T(8,128)(2,1)} %query_w.1, bf16[512,512]{1,0:T(8,128)(2,1)} %key_w.1, ...), custom_call_target="tpu_custom_call" | custom-call | tf_op jit(solution)/shard_map/attend/pallas_call | solution.py:291
  (5 shorter events, 0.1 us)
Async XLA Ops:
  67.9 22.9 %copy-start = (s32[512,32]{0,1:T(8,128)S(1)}, s32[512,32]{0,1:T(8,128)}, u32[]{:S(2)}) copy-start(s32[512,32]{0,1:T(8,128)} %param.24) | copy-start | bytes 196612

commit v2 on v1

v2 whole, which is shorter than its diff:
```python
import functools
import math

import jax
import jax.numpy as jnp
from jax import lax
from jax.experimental import pallas as pl
from jax.experimental.pallas import tpu as pltpu
from jax.sharding import PartitionSpec as P

HEADS = 4
REACH = 2
SLOTS = 2 * REACH + 1
LANES = 128
GROUP = 8
GRID_CHUNKS = 8
MESH_CHUNKS = 4

norm_eps = 1e-05
head_eps = 1e-06
BF = jnp.bfloat16
F32 = jnp.float32


def dot(a, b):
    return jnp.dot(a, b, preferred_element_type=F32)


def dot_nt(a, b):
    return lax.dot_general(a, b, (((1,), (1,)), ((), ())), preferred_element_type=F32)


def silu(v):
    return v / (1.0 + jnp.exp(-v))


def rms_scale(values, gain):
    square = jnp.mean(values * values, axis=-1, keepdims=True)
    return (values * lax.rsqrt(square + norm_eps) * gain).astype(BF)


class Relay:
    def __init__(self, count, parts, srcs, wins, send, recv, local):
        self.srcs, self.wins, self.send, self.recv, self.local = srcs, wins, send, recv, local
        me = lax.axis_index("patch")
        core = me % 2
        chip_odd = (me // 2) % 2
        self.core = core
        self.partner = me + 1 - 2 * core
        self.mate = me + 2 - 4 * chip_odd
        self.far = (me + 4 - 8 * chip_odd + count) % count
        self.far_from = (me - 4 + 8 * chip_odd + count) % count
        self.mate_slot = 4 - 4 * chip_odd
        self.far_slot = 4 * chip_odd
        self.partner_slot = 3 - 2 * core
        self.passed_slot = 1 + 2 * core
        self.pieces = []
        for a, part in enumerate(parts):
            rows = srcs[a].shape[0] // part
            for c in range(part):
                self.pieces.append((a, c * rows, rows))
        self.total = len(self.pieces)
        self.onward, self.passed = [], []

    def remote(self, src, dst, sem, other):
        return pltpu.make_async_remote_copy(
            src_ref=src,
            dst_ref=dst,
            send_sem=self.send.at[sem],
            recv_sem=self.recv.at[sem],
            device_id={"patch": other},
            device_id_type=pl.DeviceIdType.MESH,
        )

    def start(self):
        barrier = pltpu.get_barrier_semaphore()
        for other in (self.partner, self.mate, self.far, self.far_from):
            pl.semaphore_signal(
                barrier, inc=1, device_id={"patch": other}, device_id_type=pl.DeviceIdType.MESH
            )
        pl.semaphore_wait(barrier, 4)
        self.to_mate, self.to_partner = [], []
        for i, (a, r, n) in enumerate(self.pieces):
            src, win = self.srcs[a].at[pl.ds(r, n)], self.wins[a]
            self.to_mate.append(
                self.remote(src, win.at[self.far_slot, pl.ds(r, n)], i, self.mate)
            )
            self.to_mate[-1].start()
        for i, (a, r, n) in enumerate(self.pieces):
            src, win = self.srcs[a].at[pl.ds(r, n)], self.wins[a]
            self.to_partner.append(
                self.remote(
                    src, win.at[self.passed_slot, pl.ds(r, n)], self.total + i, self.partner
                )
            )
            self.to_partner[-1].start()

    def relay(self, i):
        a, r, n = self.pieces[i]
        win = self.wins[a]
        self.to_mate[i].wait_recv()
        self.onward.append(
            self.remote(
                win.at[self.mate_slot, pl.ds(r, n)],
                win.at[self.far_slot, pl.ds(r, n)],
                2 * self.total + i,
                self.far,
            )
        )
        self.onward[i].start()

    def hand_over(self, i):
        a, r, n = self.pieces[i]
        win = self.wins[a]
        self.onward[i].wait_recv()
        self.passed.append(
            self.remote(
                win.at[4 - 4 * self.core, pl.ds(r, n)],
                win.at[self.partner_slot, pl.ds(r, n)],
                3 * self.total + i,
                self.partner,
            )
        )
        self.passed[i].start()

    def finish(self):
        for copy in self.to_mate + self.to_partner + self.onward + self.passed:
            copy.wait_send()


def column(row):
    return jnp.transpose(jnp.broadcast_to(row, (LANES, LANES)))


def pick_matrix(row, size):
    lane = lax.broadcasted_iota(jnp.int32, (LANES, LANES), 1)
    blocks = []
    for e in range(0, row.shape[1], LANES):
        ids = column(row[:, e : e + LANES])
        blocks.append(
            jnp.concatenate(
                [jnp.where(ids == lane + t, 1.0, 0.0).astype(BF) for t in range(0, size, LANES)],
                axis=1,
            )
        )
    return jnp.concatenate(blocks, axis=0)


def encode_body(
    count, grid, ends, mesh, bias, gain, grid_w_in, mesh_w_in, msg_w_in, agg_w_in, upd_w_in,
    out_w_in, encoded_ref, normed_ref,
    window, end_window, table, node_table, summed,
    grid_w, mesh_w, msg_w, agg_w, upd_w, out_w, send, recv, local,
):
    loads = []
    pairs = (
        (grid_w_in, grid_w), (mesh_w_in, mesh_w), (msg_w_in, msg_w), (agg_w_in, agg_w),
        (upd_w_in, upd_w), (out_w_in, out_w), (ends, end_window.at[REACH]),
    )
    for i, (source, target) in enumerate(pairs):
        loads.append(pltpu.make_async_copy(source, target, local.at[i]))
        loads[-1].start()
    relay = Relay(count, (1, GRID_CHUNKS), (ends, grid), (end_window, window), send, recv, local)
    relay.start()
    for load in loads:
        load.wait()
    nodes = mesh.shape[0]
    edges = ends.shape[1]
    half = edges // 2
    rows = grid.shape[0] // GRID_CHUNKS
    node_table[...] = dot(mesh[...], mesh_w[...]).astype(BF)
    summed[...] = jnp.zeros(summed.shape, F32)

    def project(slot, block, r):
        table[slot, pl.ds(r, block.shape[0]), :] = (dot(block, grid_w[...]) + bias[...]).astype(BF)

    def hop(slot, between):
        sends = end_window[slot, pl.ds(SLOTS - 1 - slot, 1), :]
        recvs = end_window[slot, pl.ds(2 * SLOTS - 1 - slot, 1), :]
        messages = []
        for e in (0, half):
            pick_s = pick_matrix(sends[:, e : e + half], grid.shape[0])
            pick_r = pick_matrix(recvs[:, e : e + half], nodes)
            both = dot(pick_s, table[slot]) + dot(pick_r, node_table[...])
            messages.append(dot(silu(both).astype(BF), msg_w[...]).astype(BF))
            between()
        message = jnp.concatenate(messages, axis=0)
        row = lax.broadcasted_iota(jnp.int32, (nodes, edges), 0)
        spread = jnp.where(recvs == row, 1.0, 0.0).astype(BF)
        summed[...] += dot(spread, message)

    pumped = [0]

    def pump():
        i = pumped[0]
        relay.relay(i)
        if i > 0:
            r = relay.pieces[i][1]
            project(relay.mate_slot, window[relay.mate_slot, pl.ds(r, rows), :], r)
        pumped[0] += 1

    def idle():
        return None

    project(REACH, grid[...], 0)
    hop(REACH, pump)
    for copy in relay.to_partner:
        copy.wait_recv()
    project(relay.partner_slot, window[relay.partner_slot], 0)
    hop(relay.partner_slot, pump)
    while pumped[0] < relay.total:
        pump()

    handed = [0]

    def hand():
        i = handed[0]
        relay.hand_over(i)
        if i > 0:
            r = relay.pieces[i][1]
            project(relay.far_slot, window[relay.far_slot, pl.ds(r, rows), :], r)
        handed[0] += 1

    def hand_some():
        for _ in range(3):
            hand()

    hop(relay.mate_slot, hand_some)
    while handed[0] < relay.total:
        hand()
    hop(relay.far_slot, idle)
    for copy in relay.passed:
        copy.wait_recv()
    project(relay.passed_slot, window[relay.passed_slot], 0)
    hop(relay.passed_slot, idle)

    aggregate = summed[...].astype(BF)
    update = silu(dot(aggregate, agg_w[...]) + dot(mesh[...], upd_w[...])).astype(BF)
    encoded = mesh[...].astype(F32) + dot(update, out_w[...])
    encoded_ref[...] = encoded
    normed_ref[...] = rms_scale(encoded, gain[...])
    relay.finish()


def attend_body(
    count, normed_in, encoded, code, low, gain, query_w_in, key_w_in, value_w_in, out_w_in, in_w_in,
    ffn_w_in, result,
    window, counts, queries, keys, values, key_scale, attended,
    query_w, key_w, value_w, out_w, in_w, ffn_w, send, recv, local,
):
    nodes, width = encoded.shape
    head = width // HEADS
    span = SLOTS * nodes
    tiles = span // LANES
    loads = []
    pairs = (
        (query_w_in, query_w), (key_w_in, key_w), (value_w_in, value_w), (out_w_in, out_w),
        (in_w_in, in_w), (ffn_w_in, ffn_w),
    )
    for i, (source, target) in enumerate(pairs):
        loads.append(pltpu.make_async_copy(source, target, local.at[i]))
        loads[-1].start()
    relay = Relay(count, (MESH_CHUNKS,), (normed_in,), (window,), send, recv, local)
    relay.start()

    def project(slot, block):
        rows = pl.ds(pl.multiple_of(slot * nodes, nodes), nodes)
        k = dot(block, key_w[...]).astype(BF)
        keys[rows, :] = k
        values[rows, :] = dot(block, value_w[...]).astype(BF)
        wide = k.astype(F32)
        square = wide * wide
        upper = square.astype(BF)
        lower = (square - upper.astype(F32)).astype(BF)
        pick_row = lax.broadcasted_iota(jnp.int32, (GROUP, width), 0)
        pick_lane = lax.broadcasted_iota(jnp.int32, (GROUP, width), 1)
        pick = jnp.where(pick_lane // head == pick_row, 1.0, 0.0).astype(BF)
        sums = dot_nt(pick, upper) + dot_nt(pick, lower)
        key_scale[slot] = lax.rsqrt(sums / head + head_eps)

    def count_group(g, carry):
        left_row = lax.broadcasted_iota(jnp.int32, (tiles * GROUP, code.shape[2]), 0)
        right_row = lax.broadcasted_iota(jnp.int32, (LANES, code.shape[2]), 0)
        left = jnp.where(code[g] == left_row, 1.0, 0.0).astype(BF)
        right = jnp.where(low[g] == right_row, 1.0, 0.0).astype(BF)
        found = dot_nt(left, right)
        rows = pl.ds(pl.multiple_of(g * GROUP, GROUP), GROUP)
        for t in range(tiles):
            counts[rows, t * LANES : (t + 1) * LANES] = found[t * GROUP : (t + 1) * GROUP, :]
        return carry

    groups = nodes // GROUP
    for load in loads[:3]:
        load.wait()
    queries[...] = dot(normed_in[...], query_w[...]).astype(BF)
    project(REACH, normed_in[...])
    for i in range(MESH_CHUNKS):
        first, last = i * groups // MESH_CHUNKS, (i + 1) * groups // MESH_CHUNKS
        lax.fori_loop(first, last, count_group, 0, unroll=2)
        relay.relay(i)
    for copy in relay.to_partner:
        copy.wait_recv()
    project(relay.partner_slot, window[relay.partner_slot])
    project(relay.mate_slot, window[relay.mate_slot])
    for i in range(MESH_CHUNKS):
        relay.hand_over(i)
    project(relay.far_slot, window[relay.far_slot])
    for copy in relay.passed:
        copy.wait_recv()
    project(relay.passed_slot, window[relay.passed_slot])
    for load in loads[3:]:
        load.wait()

    tile = LANES
    def attend_tile(t, carry):
        rows = pl.ds(pl.multiple_of(t * tile, tile), tile)
        for h in range(HEADS):
            cols = slice(h * head, (h + 1) * head)
            q = queries[rows, cols]
            qf = q.astype(F32)
            q_scale = lax.rsqrt(jnp.sum(qf * qf, axis=1, keepdims=True) / head + head_eps)
            q_scale = q_scale * (1.0 / math.sqrt(head))
            k_scale = jnp.concatenate([key_scale[s, h : h + 1, :] for s in range(SLOTS)], axis=1)
            scores = dot_nt(q, keys[:, cols]) * q_scale * k_scale
            exponent = jnp.exp(scores)
            c = counts[rows, :]
            inverse = 1.0 / jnp.sum(exponent * c, axis=1, keepdims=True)
            weight = (exponent * inverse).astype(BF).astype(F32)
            mixed = dot((weight * c).astype(BF), values[:, cols])
            attended[rows, cols] = mixed.astype(BF)
        return carry

    lax.fori_loop(0, nodes // tile, attend_tile, 0)

    hidden = encoded[...] + dot(attended[...], out_w[...])
    normed = rms_scale(hidden, gain[...])
    wide = in_w.shape[1]
    step = wide // 4
    total = hidden
    for f in range(0, wide, step):
        expanded = silu(dot(normed, in_w[:, f : f + step])).astype(BF)
        total = total + dot(expanded, ffn_w[f : f + step, :])
    result[...] = total.astype(BF)
    relay.finish()


def shards(
    grid_latents, mesh_latents, enc_send, enc_recv, neighbours, enc_grid_w, enc_bias, enc_mesh_w,
    enc_msg_w, upd_agg_w, upd_mesh_w, upd_out_w, norm_gain, query_w, key_w, value_w, out_w,
    ffn_gain, ffn_in_w, ffn_out_w,
):
    count = lax.axis_size("patch")
    nodes, width = mesh_latents.shape
    own_index = lax.axis_index("patch")
    blocks = enc_send.shape[0] // SLOTS
    edges = blocks * enc_send.shape[1]
    vmem = pl.BlockSpec(memory_space=pltpu.VMEM)
    hbm = pl.BlockSpec(memory_space=pl.ANY)

    def like(a):
        return pltpu.VMEM(a.shape, a.dtype)

    def dma(n):
        return pltpu.SemaphoreType.DMA((n,))

    def params(collective_id):
        return pltpu.CompilerParams(
            vmem_limit_bytes=60 * 1024 * 1024, collective_id=collective_id, has_side_effects=True
        )

    ends = jnp.concatenate([enc_send.reshape(SLOTS, edges), enc_recv.reshape(SLOTS, edges)], axis=0)
    ends = jnp.pad(ends, ((0, 16 - 2 * SLOTS), (0, 0)))
    weights = (enc_grid_w, enc_mesh_w, enc_msg_w, upd_agg_w, upd_mesh_w, upd_out_w)
    grid_rows = grid_latents.shape[0]
    pieces = 4 * (1 + GRID_CHUNKS)
    encoded, normed = pl.pallas_call(
        functools.partial(encode_body, count),
        out_shape=[
            jax.ShapeDtypeStruct((nodes, width), F32),
            jax.ShapeDtypeStruct((nodes, width), BF),
        ],
        in_specs=[vmem] * 5 + [hbm] * 6,
        out_specs=[vmem] * 2,
        scratch_shapes=[
            pltpu.VMEM((SLOTS, grid_rows, width), BF),
            pltpu.VMEM((SLOTS,) + ends.shape, jnp.int32),
            pltpu.VMEM((SLOTS, grid_rows, width), BF),
            pltpu.VMEM((nodes, width), BF),
            pltpu.VMEM((nodes, width), F32),
        ]
        + [like(w) for w in weights]
        + [dma(pieces), dma(pieces), dma(7)],
        compiler_params=params(0),
        name="encode",
    )(grid_latents, ends, mesh_latents, enc_bias[None, :], norm_gain[None, :], *weights)

    owners = neighbours // nodes
    position = (owners - own_index + REACH) % count * nodes + neighbours % nodes
    lane = jnp.arange(nodes, dtype=jnp.int32)[:, None] % GROUP
    packed = (nodes // GROUP, 1, GROUP * neighbours.shape[1])
    code = (position // LANES * GROUP + lane).reshape(packed)
    low = (position % LANES).reshape(packed)
    weights = (query_w, key_w, value_w, out_w, ffn_in_w, ffn_out_w)
    pieces = 4 * MESH_CHUNKS
    return pl.pallas_call(
        functools.partial(attend_body, count),
        out_shape=jax.ShapeDtypeStruct((nodes, width), BF),
        in_specs=[vmem] * 5 + [hbm] * 6,
        out_specs=vmem,
        scratch_shapes=[
            pltpu.VMEM((SLOTS, nodes, width), BF),
            pltpu.VMEM((nodes, SLOTS * nodes), F32),
            pltpu.VMEM((nodes, width), BF),
            pltpu.VMEM((SLOTS * nodes, width), BF),
            pltpu.VMEM((SLOTS * nodes, width), BF),
            pltpu.VMEM((SLOTS, GROUP, nodes), F32),
            pltpu.VMEM((nodes, width), BF),
        ]
        + [like(w) for w in weights]
        + [dma(pieces), dma(pieces), dma(6)],
        compiler_params=params(1),
        name="attend",
    )(normed, encoded, code, low, ffn_gain[None, :], *weights)


def solution(mesh):
    rows = P(("groups", "patch"), None)
    in_specs = (rows,) * 5 + (P(),) * 15
    return jax.shard_map(shards, mesh=mesh, in_specs=in_specs, out_specs=rows, check_vma=False)
```

time: 126 us -> 90.3 us (0.72)
  Pallas kernels: 116 us -> 83.1 us
  local copies, waits for them, and re-layouts: 8.47 us -> 5.73 us
    pallas_call x4 -> x2, Pallas kernels: 116 us -> 83.1 us  [the longest x1 42.5 us: shards(): pl.pallas_call(functools.partial(encode_body, count), out_shape=[jax.Shap...]
    broadcast_in_dim x3 -> x0, local copies, waits for them, and re-layouts: 3.66 us -> none  [the longest x1 1.55 us: shards(): sends[:, :, None]]
    unnamed x2 -> x1, local copies, waits for them, and re-layouts: 0.01 us -> 1.87 us
where the time goes in v2:
time: 90.3 us; the launch traced here: 89.9 us
  Pallas kernels  83.1 us (92%)
  local copies, waits for them, and re-layouts  5.73 us (6%)
  other arithmetic  1.02 us (1%)
    pallas_call x1, Pallas kernels, shards(): pl.pallas_call(functools.partial(encode_body, count), out_shape=[jax.Shap...  42.5 us
    pallas_call x1, Pallas kernels, shards(): pl.pallas_call(functools.partial(attend_body, count), out_shape=jax.Shape...  40.6 us
    unnamed x1, local copies, waits for them, and re-layouts  1.87 us

profile of v2, /device:TPU:1, one launch (start us, length us, event | category | flops | bytes accessed | tf_op | source)
XLA Modules:
  0.0 89.9 jit_solution(14150174713059413634)
XLA Ops:
  0.0 0.7 reshape.27
  0.7 0.7 reshape.28
  1.4 0.6 pad.4.ends
  2.0 1.0 %add_select_fusion = (s32[512,32]{0,1:T(8,128)S(1)}, s32[512,32]{0,1:T(8,128)S(1)}) fusion(s32[]{:T(128)S(6)} %axis_index.12, s32[512,32]{0,1:T(8,128)} %param.24), kind=kLoop, calls=%fused_computation | loop fusion | flops 737280 | bytes 196612 | tf_op jit(solution)/shard_map/jit(remainder)/select_n | solution.py:402
  3.1 0.1 copy.23
  3.2 0.8 reshape.31.code
  4.0 0.1 copy.24
  4.1 0.8 reshape.32.low
  4.9 42.5 %encode.1 = (f32[512,512]{1,0:T(8,128)}, bf16[512,512]{1,0:T(8,128)(2,1)}) custom-call(bf16[1024,512]{1,0:T(8,128)(2,1)} %grid.1, s32[16,512]{1,0:T(8,128)} %pad.4.ends, bf16[512,512]{1,0:T(8,128)(2,1)} %mesh.1, f32[1,512]{1,0:T(1,128)} %bitcast.3, f32[1,512]{1,0:T(1,128)} %bitcast.4, bf16[512,512]{1,0:T(8,128)(2,1)} %grid_w_in.1, ...), custom_call_target="tpu_custom_call" | custom-call | tf_op jit(solution)/shard_map/encode/pallas_call | solution.py:376
  47.4 40.6 %attend.1 = bf16[512,512]{1,0:T(8,128)(2,1)} custom-call(bf16[512,512]{1,0:T(8,128)(2,1)} %get-tuple-element.7.normed_in, f32[512,512]{1,0:T(8,128)} %get-tuple-element.8.encoded, s32[64,1,256]{2,1,0:T(1,128)} %reshape.31.code, s32[64,1,256]{2,1,0:T(1,128)} %reshape.32.low, f32[1,512]{1,0:T(1,128)} %bitcast.5, bf16[512,512]{1,0:T(8,128)(2,1)} %query_w_in.1, ...), custom_call_target="tpu_custom_call" | custom-call | tf_op jit(solution)/shard_map/attend/pallas_call | solution.py:405
  88.0 1.9 %copy.28 = bf16[512,512]{1,0:T(8,128)(2,1)} copy(bf16[512,512]{1,0:T(8,128)(2,1)} %attend.1) | data formatting | bytes 1048576
  (3 shorter events, 0.1 us)
